TPU v7x, 256 devices: a whole 4x4x8 slice. The times are simulated.
256 devices in a mesh: section: 16 (over z, x_lo), fsdp: 16 (over x_hi, y, core).
Axes of the slice: x: 4 (x_hi: 2, x_lo: 2; x = x_hi * 2 + x_lo), y: 4, z: 8, core: 2. Of those that a mesh axis runs over, the one named last changes fastest.
Arguments:
- layer_inputs: bfloat16 [16, 2, 6144, 2048], P('section', None, 'fsdp'), may hold values from -6 to 6
- out_grads: bfloat16 [16, 2, 6144, 2048], P('section', None, 'fsdp'), may hold values from -6 to 6
- attn_stash: bfloat16 [16, 2, 6144, 1024], P('section', None, 'fsdp'), may hold values from -6 to 6
- proj_grads: bfloat16 [16, 2, 6144, 1536], P('section', None, 'fsdp'), may hold values from -6 to 6
- w_qkv: bfloat16 [16, 2048, 1536], P('section', 'fsdp'), may hold values from -0.125 to 0.125
- w_out: bfloat16 [16, 1024, 2048], P('section', 'fsdp'), may hold values from -0.1875 to 0.1875
- norm_gain: float32 [16, 2048], P('section'), may hold values from 0.25 to 1.75
- b_sched: int32 [16], P('section'), may hold values from 0 to 1
- w_sched: int32 [16], P('section'), may hold values from 0 to 1
Outputs:
- prev_grads: bfloat16 [16, 6144, 2048], P('section', 'fsdp')
- grad_qkv: float32 [16, 2048, 1536], P('section', 'fsdp')
- grad_out: float32 [16, 1024, 2048], P('section', 'fsdp')
All inputs are finite; a program needn't handle non-finite values.
Results may differ from a plain program's by a relative error of at most 0.012.
Values may be sent and summed in bfloat16 or wider, within the bound.
No kernel may reach another device: no remote copies, remote signals or barrier semaphores. Data moves between devices by JAX's collectives and lax.ppermute only.
A program may use at most 128 MiB of HBM per device.

v0:
```python
import jax
import jax.numpy as jnp
from jax import lax
from jax.sharding import Mesh
from jax.sharding import PartitionSpec as P

HEAD_DIM = 64
HEADS = 16
KV_HEADS = 4
FSDP = ("fsdp_0", "fsdp_1", "fsdp_2")
rms_eps = 1e-05
rope_base = 500000.0


def passed_along(array, axis, by):
    size = lax.axis_size(axis)
    return lax.ppermute(array, axis, [(i, (i + by) % size) for i in range(size)])


def cut_along(array, dim, size):
    before, after = (array.shape[:dim], array.shape[dim + 1 :])
    return jnp.moveaxis(array.reshape(*before, size, -1, *after), dim, 0)


def summed_rows(array, chips, core, dim):
    sizes = (lax.axis_size(chips), lax.axis_size(core))
    parts = cut_along(array, dim, sizes[0] * sizes[1])
    inside = parts.shape[1:]
    parts = parts.reshape(*sizes, *inside).swapaxes(0, 1).reshape(-1, *inside)
    parts = lax.psum_scatter(parts, core, scatter_dimension=0, tiled=True)
    return lax.psum_scatter(parts, chips, scatter_dimension=0, tiled=True)[0]


def rope_tables(length, head_size):
    halfway = head_size // 2
    indices = jnp.arange(halfway, dtype=jnp.float32)
    frequency = rope_base ** (-2.0 * indices / head_size)
    angles = jnp.arange(length, dtype=jnp.float32)[:, None] * frequency[None, :]
    angles = jnp.concatenate([angles, angles], axis=1)
    return (jnp.cos(angles), jnp.sin(angles))


def rotate_half(values):
    halfway = values.shape[-1] // 2
    return jnp.concatenate([-values[..., halfway:], values[..., :halfway]], axis=-1)


def apply_rope(values, cosine_table, sine_table):
    return values * cosine_table[:, None, :] + rotate_half(values) * sine_table[:, None, :]


def unapply_rope(values, cosine_table, sine_table):
    return values * cosine_table[:, None, :] - rotate_half(values * sine_table[:, None, :])


def contract(pattern, first_operand, second_operand):
    return jnp.einsum(pattern, first_operand, second_operand, preferred_element_type=jnp.float32)


def normalize(inputs, gain_values):
    widened = inputs.astype(jnp.float32)
    inv_rms = lax.rsqrt(jnp.mean(widened * widened, axis=-1, keepdims=True) + rms_eps)
    normed = (widened * inv_rms * gain_values).astype(jnp.bfloat16)
    return (widened, inv_rms, normed)


def attention_back(qkv_rows, attn_grad, cosine_table, sine_table):
    tokens_here = qkv_rows.shape[0]
    q_width = HEADS * HEAD_DIM
    kv_width = KV_HEADS * HEAD_DIM
    group_size = HEADS // KV_HEADS
    score_scale = HEAD_DIM ** (-0.5)
    queries = apply_rope(
        qkv_rows[:, :q_width].reshape(tokens_here, HEADS, HEAD_DIM), cosine_table, sine_table
    ).astype(jnp.bfloat16)
    key_heads = apply_rope(
        qkv_rows[:, q_width : q_width + kv_width].reshape(tokens_here, KV_HEADS, HEAD_DIM),
        cosine_table,
        sine_table,
    ).astype(jnp.bfloat16)
    values = (
        qkv_rows[:, q_width + kv_width :]
        .reshape(tokens_here, KV_HEADS, HEAD_DIM)
        .astype(jnp.bfloat16)
    )
    queries = queries.reshape(tokens_here, KV_HEADS, group_size, HEAD_DIM)
    grad_heads = attn_grad.reshape(tokens_here, KV_HEADS, group_size, HEAD_DIM)
    scores = contract("tkgd,ukd->kgtu", queries, key_heads) * score_scale
    row_ids = lax.broadcasted_iota(jnp.int32, (tokens_here, tokens_here), 0)
    col_ids = lax.broadcasted_iota(jnp.int32, (tokens_here, tokens_here), 1)
    causal = col_ids <= row_ids
    exp_scores = jnp.where(causal, jnp.exp(scores), 0.0)
    attention = exp_scores / jnp.sum(exp_scores, axis=-1, keepdims=True)
    attention_low = attention.astype(jnp.bfloat16)
    grad_values = contract("kgtu,tkgd->ukd", attention_low, grad_heads)
    grad_attention = contract("tkgd,ukd->kgtu", grad_heads, values)
    row_delta = jnp.sum(attention * grad_attention, axis=-1, keepdims=True)
    grad_scores = (attention * (grad_attention - row_delta) * score_scale).astype(jnp.bfloat16)
    grad_queries = contract("kgtu,ukd->tkgd", grad_scores, key_heads)
    grad_keys = contract("kgtu,tkgd->ukd", grad_scores, queries)
    grad_queries = unapply_rope(
        grad_queries.reshape(tokens_here, HEADS, HEAD_DIM), cosine_table, sine_table
    )
    grad_keys = unapply_rope(grad_keys, cosine_table, sine_table)
    joined = jnp.concatenate(
        [
            grad_queries.reshape(tokens_here, q_width),
            grad_keys.reshape(tokens_here, kv_width),
            grad_values.reshape(tokens_here, kv_width),
        ],
        axis=1,
    )
    return joined.astype(jnp.bfloat16)


def finish_grad(widened, inv_rms, gain_values, upstream, grad_normed):
    scaled = grad_normed * gain_values
    inner_mean = jnp.mean(scaled * widened, axis=-1, keepdims=True)
    result = upstream.astype(jnp.float32) + inv_rms * scaled - widened * inv_rms**3 * inner_mean
    return result.astype(jnp.bfloat16)


def local(
    layer_inputs, out_grads, attn_stash, proj_grads, w_qkv, w_out, norm_gain, b_sched, w_sched
):
    seq_len = layer_inputs.shape[2]
    cosine_table, sine_table = rope_tables(seq_len, HEAD_DIM)
    gain_values = norm_gain[0]
    b_slot = b_sched[0]
    w_slot = w_sched[0]
    qkv_shard = w_qkv[0]
    out_shard = w_out[0]
    contract_rows = (((0,), (0,)), ((), ()))
    contract_cols = (((1,), (1,)), ((), ()))
    inputs_b = lax.dynamic_index_in_dim(layer_inputs[0], b_slot, 0, keepdims=False)
    upstream_b = lax.dynamic_index_in_dim(out_grads[0], b_slot, 0, keepdims=False)
    widened, inv_rms, normed = normalize(inputs_b, gain_values)
    whole_qkv = lax.all_gather(qkv_shard, FSDP, axis=0, tiled=True)
    qkv_rows = jnp.dot(normed, whole_qkv, preferred_element_type=jnp.float32)
    attn_grad = lax.dot_general(
        upstream_b,
        lax.all_gather(out_shard, FSDP, axis=0, tiled=True),
        contract_cols,
        preferred_element_type=jnp.float32,
    ).astype(jnp.bfloat16)
    grad_proj = attention_back(qkv_rows, attn_grad, cosine_table, sine_table)
    grad_normed = lax.dot_general(
        grad_proj, whole_qkv, contract_cols, preferred_element_type=jnp.float32
    )
    sent_grads = finish_grad(widened, inv_rms, gain_values, upstream_b, grad_normed)
    sent_back = passed_along(sent_grads, "section", -1)[None]
    inputs_w = lax.dynamic_index_in_dim(layer_inputs[0], w_slot, 0, keepdims=False)
    upstream_w = lax.dynamic_index_in_dim(out_grads[0], w_slot, 0, keepdims=False)
    attended_w = lax.dynamic_index_in_dim(attn_stash[0], w_slot, 0, keepdims=False)
    projected_w = lax.dynamic_index_in_dim(proj_grads[0], w_slot, 0, keepdims=False)
    unused_wide, unused_inv, normed_w = normalize(inputs_w, gain_values)
    rows_part = normed_w
    grad_qkv_w = lax.psum_scatter(
        lax.dot_general(
            rows_part, projected_w, contract_rows, preferred_element_type=jnp.float32
        ).astype(jnp.bfloat16),
        FSDP,
        scatter_dimension=0,
        tiled=True,
    ).astype(jnp.float32)
    rows_part = attended_w
    grad_out_w = summed_rows(
        lax.dot_general(
            rows_part, upstream_w, contract_rows, preferred_element_type=jnp.float32
        ).astype(jnp.bfloat16),
        ("fsdp_0", "fsdp_1"),
        "fsdp_2",
        0,
    ).astype(jnp.float32)
    grad_qkv_w, grad_out_w = (grad_qkv_w[None], grad_out_w[None])
    return (sent_back, grad_qkv_w, grad_out_w)


def solution(mesh):
    finer = Mesh(
        mesh.devices.reshape(mesh.shape["section"], 2, 4, 2),
        ("section", "fsdp_0", "fsdp_1", "fsdp_2"),
    )
    return jax.shard_map(
        local,
        mesh=finer,
        in_specs=(
            P("section", None, FSDP, None),
            P("section", None, FSDP, None),
            P("section", None, FSDP, None),
            P("section", None, FSDP, None),
            P("section", FSDP, None),
            P("section", FSDP, None),
            P("section", None),
            P("section"),
            P("section"),
        ),
        out_specs=(P("section", FSDP, None), P("section", FSDP, None), P("section", FSDP, None)),
        check_vma=False,
    )
```

profile of v0, /device:TPU:1, one launch (start us, length us, event | category | flops | bytes accessed | tf_op | source)
XLA Modules:
  0.0 281.7 jit_solution(17291368382302800708)
XLA Ops:
  8.0 0.0 copy-start
  8.0 0.0 all-gather.7.cloned.1.call-start
  8.1 0.7 all-gather.7.cloned.1.call-update
  8.7 0.0 reduce-scatter.6.cloned.1.call-start
  9.4 4.0 %convolution_convert_fusion.1 = bf16[1024,2048]{1,0:T(8,128)(2,1)S(1)} fusion(bf16[1,2,384,2048]{3,2,1,0:T(8,128)(2,1)} %param.10, s32[]{:T(128)S(6)} %select_n.19, bf16[1,2,384,1024]{3,2,1,0:T(8,128)(2,1)} %param.11), kind=kOutput, calls=%fused_computation.27 | convolution fusion | flops 1612709888 | bytes 6554624 | tf_op jit(solution)/shard_map/dot_general | solution.py:168
  13.5 2.3 copy.33
  15.8 0.0 reduce-scatter.6.cloned.1.call-update
  15.8 0.0 all-gather.5.cloned.1.call-start
  15.9 0.7 all-gather.5.cloned.1.call-update
  16.6 0.0 reduce-scatter.4.cloned.1.call-start
  16.6 1.8 fusion.17
  18.4 7.2 %convolution_convert_fusion = bf16[2048,1536]{1,0:T(8,128)(2,1)} fusion(f32[2048]{0:T(1024)S(1)} %bitcast.182, f32[384]{0:T(512)S(1)} %add_rsqrt_fusion, bf16[1,2,384,2048]{3,2,1,0:T(8,128)(2,1)} %param.9, s32[]{:T(128)S(6)} %select_n.19, bf16[1,2,384,1536]{3,2,1,0:T(8,128)(2,1)S(1)} %copy-done), kind=kOutput, calls=%fused_computation.9 | convolution fusion | flops 2422210560 | bytes 9055232 | tf_op jit(solution)/shard_map/dot_general | solution.py:159
  25.6 0.0 reduce-scatter.4.cloned.1.call-update
  25.7 0.0 reduce-scatter.8.cloned.1.call-start
  26.4 1.8 fusion.20
  28.2 0.7 iota_compare_fusion
  28.9 0.1 iota_multiply_fusion
  29.0 0.9 fusion.74
  29.9 45.8 %all-gather.7.cloned.1.call-done = bf16[1,1024,2048]{2,1,0:T(8,128)(2,1)} async-done(((bf16[1,64,2048]{2,1,0:T(8,128)(2,1)}), bf16[1,1024,2048]{2,1,0:T(8,128)(2,1)}) %all-gather.7.cloned.1.call-update) | async-done | bytes 4194320 | tf_op jit(solution)/shard_map/all_gather | solution.py:142
  75.7 4.5 %fusion.45 = bf16[384,1024]{1,0:T(8,128)(2,1)S(1)} fusion(bf16[1,1024,2048]{2,1,0:T(8,128)(2,1)} %all-gather.7.cloned.1.call-done, bf16[1,2,384,2048]{3,2,1,0:T(8,128)(2,1)} %param.10, s32[]{:T(128)S(6)} %select_n.17), kind=kOutput, calls=%fused_computation.56 | convolution fusion | flops 1611005952 | bytes 6553604 | tf_op jit(solution)/shard_map/dot_general | solution.py:140
  80.1 0.4 copy.29
  80.5 0.0 reduce-scatter.6.cloned.1.call-done
  80.5 0.0 reduce-scatter.8.cloned.1.call-update
  80.6 79.5 %all-gather.5.cloned.1.call-done = bf16[1,2048,1536]{2,1,0:T(8,128)(2,1)} async-done(((bf16[1,128,1536]{2,1,0:T(8,128)(2,1)}), bf16[1,2048,1536]{2,1,0:T(8,128)(2,1)}) %all-gather.5.cloned.1.call-update) | async-done | bytes 6291472 | tf_op jit(solution)/shard_map/all_gather | solution.py:138
  160.1 5.3 %fusion.8 = f32[384,1536]{1,0:T(8,128)S(1)} fusion(bf16[1,2048,1536]{2,1,0:T(8,128)(2,1)} %all-gather.5.cloned.1.call-done, f32[2048]{0:T(1024)S(1)} %bitcast.183, f32[384]{0:T(512)S(1)} %get-tuple-element.14, bf16[1,2,384,2048]{3,2,1,0:T(8,128)(2,1)} %param.9, s32[]{:T(128)S(6)} %select_n.17), kind=kOutput, calls=%fused_computation.12 | convolution fusion | flops 2419064832 | bytes 10233348 | tf_op jit(solution)/shard_map/dot_general | solution.py:139
  165.4 1.3 slice.48
  166.7 0.7 slice.61
  167.4 0.2 copy.25
  167.5 0.8 slice_negate_fusion.3
  168.3 1.9 copy.26
  170.2 1.0 slice_negate_fusion.1
  171.2 1.7 copy.28
  173.0 0.0 copy-start.4
  173.0 6.1 %fusion.89 = f32[4,384,384,4]{2,1,3,0:T(8,128)} fusion(bf16[384,4,64,1]{0,2,3,1:T(8,128)(2,1)} %bitcast.178, bf16[384,4,4,64]{0,3,2,1:T(8,128)(2,1)S(1)} %bitcast.171), kind=kOutput, calls=%fused_computation.104 | convolution fusion | flops 301989888 | bytes 10420224 | tf_op jit(solution)/shard_map/tkgd,ukd->kgtu/dot_general | solution.py:57
  179.1 0.0 copy-done.10
  179.1 0.1 fusion.72
  179.2 0.0 copy-start.13
  179.2 0.3 fusion.34
  179.5 0.5 copy-done.15
  180.0 5.8 %fusion.5 = (f32[4,4,384]{2,1,0:T(4,128)S(1)}, f32[4,384,384,4]{2,1,3,0:T(8,128)}) fusion(pred[384,384]{0,1:T(8,128)(4,1)S(1)} %copy-done.15, bf16[384,4,64,1]{0,2,3,1:T(8,128)(2,1)S(1)} %fusion.72, bf16[384,4,4,64]{0,3,2,1:T(8,128)(2,1)S(1)} %fusion.34), kind=kOutput, calls=%fused_computation.8 | convolution fusion | flops 309061632 | bytes 10592256 | tf_op jit(solution)/shard_map/tkgd,ukd->kgtu/dot_general | solution.py:57
  185.8 0.0 copy-done.13
  185.8 0.0 copy-start.14
  185.8 18.0 %broadcast_multiply_fusion = (f32[384,4,64]{0,2,1:T(8,128)S(1)}, f32[384,4,64]{0,2,1:T(8,128)S(1)}) fusion(f32[384,64]{0,1:T(8,128)S(1)} %copy-done.8, bf16[384,4,4,64]{0,3,2,1:T(8,128)(2,1)} %copy-done.12, f32[4,384,384,4]{2,1,3,0:T(8,128)} %fusion.89, f32[4,4,384]{2,1,0:T(4,128)S(1)} %get-tuple-element.15, f32[4,384,384,4]{2,1,3,0:T(8,128)} %get-tuple-element.16, ...), kind=kOutput, calls=%fused_computation.85 | convolution fusion | flops 328046976 | bytes 20717568 | tf_op jit(solution)/shard_map/kgtu,tkgd->ukd/dot_general | solution.py:57
  203.8 16.2 %fusion.16 = f32[4,64,4,384]{3,1,2,0:T(8,128)} fusion(bf16[384,4,64,1]{0,2,3,1:T(8,128)(2,1)S(1)} %copy-done.14, f32[4,384,384,4]{2,1,3,0:T(8,128)} %fusion.89, f32[4,384,384,4]{2,1,3,0:T(8,128)} %get-tuple-element.16, f32[4,4,384]{2,1,0:T(4,128)S(1)} %get-tuple-element.15, pred[384,384]{0,1:T(8,128)(4,1)S(1)} %copy-done.16), kind=kOutput, calls=%fused_computation.24 | convolution fusion | flops 327948672 | bytes 20815872 | tf_op jit(solution)/shard_map/kgtu,ukd->tkgd/dot_general | solution.py:57
  220.1 1.5 bitcast_multiply_fusion.8
  221.6 0.0 copy-start.3
  221.6 0.0 copy-start.6
  221.6 0.1 slice_negate_fusion
  221.8 0.1 pad_maximum_fusion
  221.9 1.2 copy-done.3
  223.0 0.3 fusion.36
  223.3 0.1 fusion.71
  223.4 0.0 copy-start.2
  223.4 0.0 slice-start.1
  223.4 6.2 %fusion.63 = bf16[4,64,384]{2,1,0:T(8,128)(2,1)S(1)} fusion(bf16[384,4,4,64]{0,3,2,1:T(8,128)(2,1)S(1)} %bitcast.172, f32[4,384,384,4]{2,1,3,0:T(8,128)} %get-tuple-element.16, f32[4,4,384]{2,1,0:T(4,128)S(1)} %get-tuple-element.15, pred[384,384]{0,1:T(8,128)(4,1)S(1)} %copy-done.16), kind=kOutput, calls=%fused_computation.68 | convolution fusion | flops 311525376 | bytes 10592256 | tf_op jit(solution)/shard_map/kgtu,tkgd->ukd/dot_general | solution.py:57
  229.7 0.0 copy-start.11
  229.7 2.8 fusion.26
  232.5 0.0 copy-start.1
  232.5 2.0 fusion.25
  234.6 3.0 %collective-permute-start = (bf16[384,2048]{1,0:T(8,128)(2,1)}, bf16[384,2048]{1,0:T(8,128)(2,1)}, u32[]{:S(2)}, u32[]{:S(2)}) collective-permute-start(bf16[384,2048]{1,0:T(8,128)(2,1)} %fusion.25), channel_id=1, source_target_pairs={{0,240},{16,0},{32,16},{48,32},{64,48},{80,64},{96,80},{112,96},{1... | collective-permute-start | bytes 4718600 | tf_op jit(solution)/shard_map/ppermute | solution.py:17
  237.6 2.0 bitcast_convert_fusion
  239.6 1.8 convert_element_type.74
  241.3 30.0 %collective-permute-done = bf16[384,2048]{1,0:T(8,128)(2,1)} collective-permute-done((bf16[384,2048]{1,0:T(8,128)(2,1)}, bf16[384,2048]{1,0:T(8,128)(2,1)}, u32[]{:S(2)}, u32[]{:S(2)}) %collective-permute-start) | collective-permute-done | bytes 1572896 | tf_op jit(solution)/shard_map/ppermute | solution.py:17
  271.4 2.7 copy.44
  (35 shorter events, 0.1 us)
Async XLA Ops:
  8.0 10.4 %copy-start = (bf16[1,2,384,1536]{3,2,1,0:T(8,128)(2,1)S(1)}, bf16[1,2,384,1536]{3,2,1,0:T(8,128)(2,1)}, u32[]{:S(2)}) copy-start(bf16[1,2,384,1536]{3,2,1,0:T(8,128)(2,1)} %param.12) | copy-start | bytes 7077892
  8.0 67.6 %all-gather.7.cloned.1.call-start = ((), (), s32[]{:S(2)}) async-start(), calls=%async_computation.7 | async-start | bytes 4456448 | tf_op jit(solution)/shard_map/all_gather | solution.py:142
  8.7 71.8 %reduce-scatter.6.cloned.1.call-start = ((), (), s32[]{:S(2)}) async-start(), calls=%async_computation.4 | async-start | bytes 6291456 | tf_op jit(solution)/shard_map/reduce_scatter | solution.py:30
  15.8 2.6 copy-start.17
  15.8 144.3 %all-gather.5.cloned.1.call-start = ((), (), s32[]{:S(2)}) async-start(), calls=%async_computation.6 | async-start | bytes 6684672 | tf_op jit(solution)/shard_map/all_gather | solution.py:138
  16.6 221.0 %reduce-scatter.4.cloned.1.call-start = ((), (), s32[]{:S(2)}) async-start(), calls=%async_computation.3 | async-start | bytes 6684672 | tf_op jit(solution)/shard_map/reduce_scatter | solution.py:158
  25.7 213.9 %reduce-scatter.8.cloned.1.call-start = ((), (), s32[]{:S(2)}) async-start(), calls=%async_computation.5 | async-start | bytes 2359296 | tf_op jit(solution)/shard_map/reduce_scatter | solution.py:31
  173.0 6.2 %copy-start.5 = (f32[384,64]{0,1:T(8,128)S(1)}, f32[384,64]{0,1:T(8,128)}, u32[]{:S(2)}) copy-start(f32[384,64]{0,1:T(8,128)} %get-tuple-element.11) | copy-start | bytes 294916
  173.0 6.2 %copy-start.7 = (f32[384,64]{0,1:T(8,128)S(1)}, f32[384,64]{0,1:T(8,128)}, u32[]{:S(2)}) copy-start(f32[384,64]{0,1:T(8,128)} %get-tuple-element.12) | copy-start | bytes 294916
  173.0 6.2 %copy-start.9 = (f32[384,4,32]{0,2,1:T(8,128)S(1)}, f32[384,4,32]{0,2,1:T(8,128)}, u32[]{:S(2)}) copy-start(f32[384,4,32]{0,2,1:T(8,128)} %get-tuple-element.9) | copy-start | bytes 589828
  173.0 6.2 %copy-start.10 = (f32[384,4,32]{0,2,1:T(8,128)S(1)}, f32[384,4,32]{0,2,1:T(8,128)}, u32[]{:S(2)}) copy-start(f32[384,4,32]{0,2,1:T(8,128)} %get-tuple-element.10) | copy-start | bytes 589828
  173.0 6.2 %copy-start.4 = (f32[384,16,32]{0,2,1:T(8,128)S(1)}, f32[384,16,32]{0,2,1:T(8,128)}, u32[]{:S(2)}) copy-start(f32[384,16,32]{0,2,1:T(8,128)} %get-tuple-element.6) | copy-start | bytes 2359300
  179.1 0.9 copy-start.15
  179.2 6.6 %copy-start.13 = (bf16[384,4,64,1]{0,2,3,1:T(8,128)(2,1)}, bf16[384,4,64,1]{0,2,3,1:T(8,128)(2,1)S(1)}, u32[]{:S(2)}) copy-start(bf16[384,4,64,1]{0,2,3,1:T(8,128)(2,1)S(1)} %fusion.72) | copy-start | bytes 589828
  180.0 5.8 %copy-start.12 = (bf16[384,4,4,64]{0,3,2,1:T(8,128)(2,1)}, bf16[384,4,4,64]{0,3,2,1:T(8,128)(2,1)S(1)}, u32[]{:S(2)}) copy-start(bf16[384,4,4,64]{0,3,2,1:T(8,128)(2,1)S(1)} %fusion.34) | copy-start | bytes 2359300
  180.0 5.8 %copy-start.8 = (f32[384,64]{0,1:T(8,128)S(1)}, f32[384,64]{0,1:T(8,128)}, u32[]{:S(2)}) copy-start(f32[384,64]{0,1:T(8,128)} %get-tuple-element.12) | copy-start | bytes 294916
  180.0 5.8 %copy-start.16 = (pred[384,384]{0,1:T(8,128)(4,1)S(1)}, pred[384,384]{0,1:T(8,128)(4,1)}, u32[]{:S(2)}) copy-start(pred[384,384]{0,1:T(8,128)(4,1)} %iota_compare_fusion) | copy-start | bytes 442372
  185.8 18.0 %copy-start.14 = (bf16[384,4,64,1]{0,2,3,1:T(8,128)(2,1)S(1)}, bf16[384,4,64,1]{0,2,3,1:T(8,128)(2,1)}, u32[]{:S(2)}) copy-start(bf16[384,4,64,1]{0,2,3,1:T(8,128)(2,1)} %copy-done.13) | copy-start | bytes 589828
  221.6 1.4 copy-start.3
  221.6 1.4 copy-start.6
  223.0 6.6 %slice-start = ((s8[6291456]{0:T(1024)(128)(4,1)}), s8[4194304]{0:T(1024)(128)(4,1)S(1)}, s32[]{:S(2)}) async-start(s8[6291456]{0:T(1024)(128)(4,1)} %bitcast.180), calls=%async_computation.8 | async-start | bytes 8388608
  223.4 6.3 %copy-start.2 = (bf16[1,2,384,2048]{3,2,1,0:T(8,128)(2,1)S(1)}, bf16[1,2,384,2048]{3,2,1,0:T(8,128)(2,1)}, u32[]{:S(2)}) copy-start(bf16[1,2,384,2048]{3,2,1,0:T(8,128)(2,1)} %param.9) | copy-start | bytes 9437188
  223.4 6.3 %slice-start.1 = ((s8[6291456]{0:T(1024)(128)(4,1)}), s8[2097152]{0:T(1024)(128)(4,1)S(1)}, s32[]{:S(2)}) async-start(s8[6291456]{0:T(1024)(128)(4,1)} %bitcast.180), calls=%async_computation.9 | async-start | bytes 4194304
  229.7 2.8 %copy-start.11 = (bf16[1,2,384,2048]{3,2,1,0:T(8,128)(2,1)S(1)}, bf16[1,2,384,2048]{3,2,1,0:T(8,128)(2,1)}, u32[]{:S(2)}) copy-start(bf16[1,2,384,2048]{3,2,1,0:T(8,128)(2,1)} %param.10) | copy-start | bytes 9437188
  232.5 41.6 %copy-start.1 = (bf16[1,2,384,1536]{3,2,1,0:T(8,128)(2,1)S(1)}, bf16[1,2,384,1536]{3,2,1,0:T(8,128)(2,1)}, u32[]{:S(2)}) copy-start(bf16[1,2,384,1536]{3,2,1,0:T(8,128)(2,1)} %param.12) | copy-start | bytes 7077892
  234.6 36.8 %collective-permute-start = (bf16[384,2048]{1,0:T(8,128)(2,1)}, bf16[384,2048]{1,0:T(8,128)(2,1)}, u32[]{:S(2)}, u32[]{:S(2)}) collective-permute-start(bf16[384,2048]{1,0:T(8,128)(2,1)} %fusion.25), channel_id=1, source_target_pairs={{0,240},{16,0},{32,16},{48,32},{64,48},{80,64},{96,80},{112,96},{1... | collective-permute-start | bytes 4718600 | tf_op jit(solution)/shard_map/ppermute | solution.py:17
Sparse Core Ops, SparseCore 0:
  11.6 64.0 all-gather.6
  78.4 81.6 all-gather.4
Sparse Core Ops, SparseCore 1:
  15.9 21.8 reduce-scatter.5
  42.1 99.7 reduce-scatter.3
  145.7 81.1 reduce-scatter.7
where the time goes:
time: 282 us
  waiting for transfers between devices  157 us (56%)
  matrix products  76.1 us (27%)
  between operations  17.3 us (6%)
  other arithmetic  15.3 us (5%)
  local copies, waits for them, and re-layouts  12.9 us (5%)
  starting transfers between devices  3.24 us (1%)
    all_gather x1, waiting for transfers between devices, local(): whole_qkv = lax.all_gather(qkv_shard, FSDP, axis=0, tiled=True)  79.5 us
    dot_general x5, matrix products, contract(): jnp.einsum(pattern, first_operand, second_operand, preferred_element_type...  52.3 us
    all_gather x1, waiting for transfers between devices, local(): lax.all_gather(out_shard, FSDP, axis=0, tiled=True)  45.8 us
    ppermute x1, waiting for transfers between devices, passed_along(): lax.ppermute(array, axis, [(i, (i + by) % size) for i in range(size)])  30 us
    dot_general x1, matrix products, local(): lax.dot_general(rows_part, projected_w, contract_rows, preferred_element_...  7.19 us
  transfers between devices with their start and end apart: 6, of which 3 were waited for; matrix products, arithmetic and copies ran while one was open for 35% of the time, Pallas kernels for 0%

commit v1 on v0

--- a/solution.py
+++ b/solution.py
@@ -135,7 +135,9 @@
     inputs_b = lax.dynamic_index_in_dim(layer_inputs[0], b_slot, 0, keepdims=False)
     upstream_b = lax.dynamic_index_in_dim(out_grads[0], b_slot, 0, keepdims=False)
     widened, inv_rms, normed = normalize(inputs_b, gain_values)
-    whole_qkv = lax.all_gather(qkv_shard, FSDP, axis=0, tiled=True)
+    whole_qkv = jnp.concatenate(
+        lax.all_to_all(jnp.stack([qkv_shard] * lax.axis_size(FSDP)), FSDP, 0, 0), axis=0
+    )
     qkv_rows = jnp.dot(normed, whole_qkv, preferred_element_type=jnp.float32)
     attn_grad = lax.dot_general(
         upstream_b,

time: 282 us -> 323 us (1.15)
  waiting for transfers between devices: 157 us -> 193 us
  starting transfers between devices: 3.24 us -> 9.91 us
  other arithmetic: 15.3 us -> 12 us
    all_to_all x0 -> x1, waiting for transfers between devices: none -> 99 us  [local(): lax.all_to_all(jnp.stack([qkv_shard] * lax.axis_size(FSDP)), FSDP, 0, 0)]
    all_gather x1 -> x0, waiting for transfers between devices: 79.5 us -> none  [local(): whole_qkv = lax.all_gather(qkv_shard, FSDP, axis=0, tiled=True)]
    reduce_scatter x1, waiting for transfers between devices: 0.01 us -> 50.2 us  [summed_rows(): return lax.psum_scatter(parts, chips, scatter_dimension=0, tiled=True)[0]]
    all_gather x1, waiting for transfers between devices: 45.8 us -> 0.01 us  [local(): lax.all_gather(out_shard, FSDP, axis=0, tiled=True)]
    ppermute x1, waiting for transfers between devices: 30 us -> 43 us  [passed_along(): lax.ppermute(array, axis, [(i, (i + by) % size) for i in range(size)])]
    all_to_all x0 -> x1, starting transfers between devices: none -> 8.57 us  [local(): lax.all_to_all(jnp.stack([qkv_shard] * lax.axis_size(FSDP)), FSDP, 0, 0)]
    dot_general x5, matrix products: 52.3 us -> 47.3 us  [contract(): jnp.einsum(pattern, first_operand, second_operand, preferred_element_type...]
    dot_general x1, matrix products: 2.81 us -> 6.26 us  [local(): lax.dot_general(grad_proj, whole_qkv, contract_cols, preferred_element_ty...]
  transfers between devices with their start and end apart: 6 -> 6, of which waited for: 3 -> 3; matrix products, arithmetic and copies ran while one was open for 35% -> 29% of each run, Pallas kernels for 0% -> 0%
where the time goes in v1:
time: 323 us
  waiting for transfers between devices  193 us (60%)
  matrix products  75.1 us (23%)
  between operations  17.2 us (5%)
  local copies, waits for them, and re-layouts  15.3 us (5%)
  other arithmetic  12 us (4%)
  starting transfers between devices  9.91 us (3%)
    all_to_all x1, waiting for transfers between devices, local(): lax.all_to_all(jnp.stack([qkv_shard] * lax.axis_size(FSDP)), FSDP, 0, 0)  99 us
    reduce_scatter x1, waiting for transfers between devices, summed_rows(): return lax.psum_scatter(parts, chips, scatter_dimension=0, tiled=True)[0]  50.2 us
    dot_general x5, matrix products, contract(): jnp.einsum(pattern, first_operand, second_operand, preferred_element_type...  47.3 us
    ppermute x1, waiting for transfers between devices, passed_along(): lax.ppermute(array, axis, [(i, (i + by) % size) for i in range(size)])  43 us
    all_to_all x1, starting transfers between devices, local(): lax.all_to_all(jnp.stack([qkv_shard] * lax.axis_size(FSDP)), FSDP, 0, 0)  8.57 us
    dot_general x1, matrix products, local(): lax.dot_general(rows_part, projected_w, contract_rows, preferred_element_...  7.62 us
  transfers between devices with their start and end apart: 6, of which 3 were waited for; matrix products, arithmetic and copies ran while one was open for 29% of the time, Pallas kernels for 0%

profile of v1, /device:TPU:1, one launch (start us, length us, event | category | flops | bytes accessed | tf_op | source)
XLA Modules:
  0.0 322.5 jit_solution(12353337983986174524)
XLA Ops:
  8.0 0.0 copy-start
  8.0 0.0 all-gather.3.cloned.1.call-start
  8.1 0.7 all-gather.3.cloned.1.call-update
  8.7 0.0 reduce-scatter.6.cloned.1.call-start
  9.4 4.0 %convolution_convert_fusion.1 = bf16[1024,2048]{1,0:T(8,128)(2,1)S(1)} fusion(bf16[1,2,384,2048]{3,2,1,0:T(8,128)(2,1)} %param.10, s32[]{:T(128)S(6)} %select_n.19, bf16[1,2,384,1024]{3,2,1,0:T(8,128)(2,1)} %param.11), kind=kOutput, calls=%fused_computation.24 | convolution fusion | flops 1612709888 | bytes 6554624 | tf_op jit(solution)/shard_map/dot_general | solution.py:170
  13.5 2.3 copy.33
  15.8 0.0 reduce-scatter.6.cloned.1.call-update
  15.8 1.0 copy-done.8
  16.8 3.3 %stack.3 = bf16[16,128,1536]{2,1,0:T(8,128)(2,1)} broadcast(bf16[128,1536]{1,0:T(8,128)(2,1)S(1)} %bitcast.186), dimensions={1,2} | broadcast | bytes 6684672 | tf_op jit(solution)/shard_map/stack | solution.py:139
  20.0 8.6 %all-to-all-start = ((bf16[16,128,1536]{2,1,0:T(8,128)(2,1)}), bf16[16,128,1536]{2,1,0:T(8,128)(2,1)}, u32[]{:S(2)}, u32[]{:S(2)}) async-start(bf16[16,128,1536]{2,1,0:T(8,128)(2,1)} %stack.3), calls=%async_computation | async-start | bytes 12582912 | tf_op jit(solution)/shard_map/all_to_all | solution.py:139
  28.6 0.0 reduce-scatter.4.cloned.1.call-start
  28.7 1.8 fusion.16
  30.5 0.0 copy-done
  30.5 0.0 copy-done.9
  30.5 7.6 %convolution_convert_fusion = bf16[2048,1536]{1,0:T(8,128)(2,1)} fusion(f32[384]{0:T(512)S(1)} %add_rsqrt_fusion, f32[2048]{0:T(1024)S(1)} %bitcast.188, bf16[1,2,384,2048]{3,2,1,0:T(8,128)(2,1)} %param.9, s32[]{:T(128)S(6)} %select_n.19, bf16[1,2,384,1536]{3,2,1,0:T(8,128)(2,1)S(1)} %copy-done), kind=kOutput, calls=%fused_computation.9 | convolution fusion | flops 2422210560 | bytes 9055232 | tf_op jit(solution)/shard_map/dot_general | solution.py:161
  38.1 0.0 reduce-scatter.4.cloned.1.call-update
  38.2 0.2 reduce-scatter.8.cloned.1.call-start
  39.0 1.8 fusion.19
  40.9 0.1 iota_multiply_fusion
  41.0 0.2 fusion.71
  41.2 99.0 %all-to-all-done = bf16[16,128,1536]{2,1,0:T(8,128)(2,1)} async-done(((bf16[16,128,1536]{2,1,0:T(8,128)(2,1)}), bf16[16,128,1536]{2,1,0:T(8,128)(2,1)}, u32[]{:S(2)}, u32[]{:S(2)}) %all-to-all-start) | async-done | bytes 6291488 | tf_op jit(solution)/shard_map/all_to_all | solution.py:139
  140.2 5.4 %fusion.27 = f32[384,1536]{1,0:T(8,128)S(1)} fusion(bf16[2048,1536]{1,0:T(8,128)(2,1)} %bitcast.6, f32[2048]{0:T(1024)S(1)} %bitcast.189, f32[384]{0:T(512)S(1)} %get-tuple-element.14, bf16[1,2,384,2048]{3,2,1,0:T(8,128)(2,1)} %param.9, s32[]{:T(128)S(6)} %select_n.17), kind=kOutput, calls=%fused_computation.37 | convolution fusion | flops 2419064832 | bytes 10233348 | tf_op jit(solution)/shard_map/dot_general | solution.py:141
  145.6 1.3 slice.48
  146.9 0.2 copy.25
  147.1 1.9 copy.26
  149.0 0.2 copy.28
  149.3 0.1 fusion.69
  149.3 0.1 slice_negate_fusion.1
  149.4 0.3 fusion.32
  149.7 0.0 copy-start.5
  149.7 0.9 copy-done.5
  150.6 5.8 %fusion.5 = (f32[4,4,384]{2,1,0:T(4,128)S(1)}, f32[4,384,384,4]{2,1,3,0:T(8,128)}) fusion(pred[384,384]{0,1:T(8,128)(4,1)S(1)} %iota_compare_fusion, bf16[384,4,64,1]{0,2,3,1:T(8,128)(2,1)S(1)} %fusion.69, bf16[384,4,4,64]{0,3,2,1:T(8,128)(2,1)S(1)} %fusion.32), kind=kOutput, calls=%fused_computation.8 | convolution fusion | flops 309061632 | bytes 10592256 | tf_op jit(solution)/shard_map/tkgd,ukd->kgtu/dot_general | solution.py:57
  156.4 4.5 %fusion.42 = bf16[384,1024]{1,0:T(8,128)(2,1)S(1)} fusion(bf16[1,1024,2048]{2,1,0:T(8,128)(2,1)} %all-gather.3.cloned.1.call-done, bf16[1,2,384,2048]{3,2,1,0:T(8,128)(2,1)} %param.10, s32[]{:T(128)S(6)} %select_n.17), kind=kOutput, calls=%fused_computation.54 | convolution fusion | flops 1611005952 | bytes 6553604 | tf_op jit(solution)/shard_map/dot_general | solution.py:142
  160.9 0.4 copy.29
  161.3 5.1 %fusion.86 = f32[4,384,384,4]{2,1,3,0:T(8,128)} fusion(bf16[384,4,64,1]{0,2,3,1:T(8,128)(2,1)S(1)} %bitcast.185, bf16[384,4,4,64]{0,3,2,1:T(8,128)(2,1)S(1)} %bitcast.178), kind=kOutput, calls=%fused_computation.102 | convolution fusion | flops 301989888 | bytes 10420224 | tf_op jit(solution)/shard_map/tkgd,ukd->kgtu/dot_general | solution.py:57
  166.3 16.2 %fusion.12 = f32[4,64,4,384]{3,1,2,0:T(8,128)} fusion(bf16[384,4,64,1]{0,2,3,1:T(8,128)(2,1)S(1)} %fusion.69, f32[4,384,384,4]{2,1,3,0:T(8,128)} %fusion.86, f32[4,384,384,4]{2,1,3,0:T(8,128)} %get-tuple-element.16, f32[4,4,384]{2,1,0:T(4,128)S(1)} %get-tuple-element.15, pred[384,384]{0,1:T(8,128)(4,1)S(1)} %iota_compare_fusion), kind=kOutput, calls=%fused_computation.16 | convolution fusion | flops 327948672 | bytes 20815872 | tf_op jit(solution)/shard_map/kgtu,ukd->tkgd/dot_general | solution.py:57
  182.5 1.5 bitcast_multiply_fusion.8
  184.0 0.0 copy-start.3
  184.0 0.1 slice_negate_fusion
  184.2 0.1 pad_maximum_fusion
  184.3 1.2 copy-done.3
  185.4 1.2 fusion.34
  186.6 6.0 %fusion.60 = bf16[4,64,384]{2,1,0:T(8,128)(2,1)S(1)} fusion(bf16[384,4,4,64]{0,3,2,1:T(8,128)(2,1)S(1)} %bitcast.179, f32[4,384,384,4]{2,1,3,0:T(8,128)} %get-tuple-element.16, f32[4,4,384]{2,1,0:T(4,128)S(1)} %get-tuple-element.15, pred[384,384]{0,1:T(8,128)(4,1)S(1)} %iota_compare_fusion), kind=kOutput, calls=%fused_computation.66 | convolution fusion | flops 311525376 | bytes 10592256 | tf_op jit(solution)/shard_map/kgtu,tkgd->ukd/dot_general | solution.py:57
  192.6 0.0 reduce-scatter.6.cloned.1.call-done
  192.7 0.0 reduce-scatter.8.cloned.1.call-update
  192.7 0.0 copy-done.6
  192.7 0.0 copy-start.7
  192.7 14.2 %broadcast_multiply_fusion = (f32[384,4,64]{0,2,1:T(8,128)S(1)}, f32[384,4,64]{0,2,1:T(8,128)S(1)}) fusion(f32[384,64]{0,1:T(8,128)S(1)} %get-tuple-element.12, bf16[384,4,4,64]{0,3,2,1:T(8,128)(2,1)S(1)} %copy-done.6, f32[4,384,384,4]{2,1,3,0:T(8,128)} %fusion.86, f32[4,4,384]{2,1,0:T(4,128)S(1)} %get-tuple-element.15, ...), kind=kOutput, calls=%fused_computation.83 | convolution fusion | flops 328046976 | bytes 20717568 | tf_op jit(solution)/shard_map/kgtu,tkgd->ukd/dot_general | solution.py:57
  207.0 0.1 fusion.68
  207.1 0.0 copy-done.7
  207.1 0.0 copy-start.2
  207.1 0.0 copy-start.4
  207.1 6.3 %fusion.23 = (f32[384]{0:T(512)S(1)}, f32[384,2048]{1,0:T(8,128)S(1)}) fusion(bf16[1,2,384,2048]{3,2,1,0:T(8,128)(2,1)} %param.9, s32[]{:T(128)S(6)} %select_n.17, f32[2048]{0:T(1024)S(1)} %bitcast.190, bf16[2048,1536]{1,0:T(8,128)(2,1)} %bitcast.6, bf16[384,256]{0,1:T(8,128)(2,1)S(1)} %bitcast.191, bf16[384,256]{0,1:T(8,128)(2,1)S(1)} %bitcast.187, ...), kind=kOutput, calls=%fused_computation.32 | convolution fusion | flops 2422603264 | bytes 12199428 | tf_op jit(solution)/shard_map/dot_general | solution.py:149
  213.4 0.0 copy-done.2
  213.4 0.0 copy-done.4
  213.4 0.0 copy-start.1
  213.4 0.8 fusion.22
  214.2 1.0 collective-permute-start
  215.2 43.0 %collective-permute-done = bf16[384,2048]{1,0:T(8,128)(2,1)} collective-permute-done((bf16[384,2048]{1,0:T(8,128)(2,1)S(1)}, bf16[384,2048]{1,0:T(8,128)(2,1)}, u32[]{:S(2)}, u32[]{:S(2)}) %collective-permute-start) | collective-permute-done | bytes 1572896 | tf_op jit(solution)/shard_map/ppermute | solution.py:17
  258.3 2.0 bitcast_convert_fusion
  260.2 50.2 %reduce-scatter.8.cloned.1.call-done = bf16[1,64,2048]{2,1,0:T(8,128)(2,1)} async-done(((bf16[8,64,2048]{2,1,0:T(8,128)(2,1)}), bf16[1,64,2048]{2,1,0:T(8,128)(2,1)}) %reduce-scatter.8.cloned.1.call-update) | async-done | bytes 262160 | tf_op jit(solution)/shard_map/reduce_scatter | solution.py:31
  310.4 1.8 convert_element_type.82
  312.2 2.7 copy.44
  314.9 0.0 copy-done.1
  (14 shorter events, 0.2 us)
Async XLA Ops:
  8.0 22.5 %copy-start = (bf16[1,2,384,1536]{3,2,1,0:T(8,128)(2,1)S(1)}, bf16[1,2,384,1536]{3,2,1,0:T(8,128)(2,1)}, u32[]{:S(2)}) copy-start(bf16[1,2,384,1536]{3,2,1,0:T(8,128)(2,1)} %param.12) | copy-start | bytes 7077892
  8.0 148.3 %all-gather.3.cloned.1.call-start = ((), (), s32[]{:S(2)}) async-start(), calls=%async_computation.7 | async-start | bytes 4456448 | tf_op jit(solution)/shard_map/all_gather | solution.py:144
  8.7 183.9 %reduce-scatter.6.cloned.1.call-start = ((), (), s32[]{:S(2)}) async-start(), calls=%async_computation.5 | async-start | bytes 6291456 | tf_op jit(solution)/shard_map/reduce_scatter | solution.py:30
  15.8 1.0 copy-start.8
  20.0 10.5 %copy-start.9 = (f32[1,2048]{1,0:T(1,128)S(1)}, f32[1,2048]{1,0:T(1,128)}, u32[]{:S(2)}) copy-start(f32[1,2048]{1,0:T(1,128)} %param.15) | copy-start | bytes 24580
  20.0 120.2 %all-to-all-start = ((bf16[16,128,1536]{2,1,0:T(8,128)(2,1)}), bf16[16,128,1536]{2,1,0:T(8,128)(2,1)}, u32[]{:S(2)}, u32[]{:S(2)}) async-start(bf16[16,128,1536]{2,1,0:T(8,128)(2,1)} %stack.3), calls=%async_computation | async-start | bytes 12582912 | tf_op jit(solution)/shard_map/all_to_all | solution.py:139
  28.6 229.7 %reduce-scatter.4.cloned.1.call-start = ((), (), s32[]{:S(2)}) async-start(), calls=%async_computation.4 | async-start | bytes 6684672 | tf_op jit(solution)/shard_map/reduce_scatter | solution.py:160
  38.2 272.3 %reduce-scatter.8.cloned.1.call-start = ((), (), s32[]{:S(2)}) async-start(), calls=%async_computation.6 | async-start | bytes 2359296 | tf_op jit(solution)/shard_map/reduce_scatter | solution.py:31
  149.7 0.9 copy-start.5
  184.0 1.4 copy-start.3
  186.6 6.1 %copy-start.6 = (bf16[384,4,4,64]{0,3,2,1:T(8,128)(2,1)S(1)}, bf16[384,4,4,64]{0,3,2,1:T(8,128)(2,1)}, u32[]{:S(2)}) copy-start(bf16[384,4,4,64]{0,3,2,1:T(8,128)(2,1)} %copy-done.5) | copy-start | bytes 2359300
  192.7 14.4 %copy-start.7 = (bf16[384,1024]{0,1:T(8,128)(2,1)S(1)}, bf16[384,1024]{0,1:T(8,128)(2,1)}, u32[]{:S(2)}) copy-start(bf16[384,1024]{0,1:T(8,128)(2,1)} %fusion.34) | copy-start | bytes 2359300
  207.1 6.3 %copy-start.2 = (bf16[1,2,384,2048]{3,2,1,0:T(8,128)(2,1)S(1)}, bf16[1,2,384,2048]{3,2,1,0:T(8,128)(2,1)}, u32[]{:S(2)}) copy-start(bf16[1,2,384,2048]{3,2,1,0:T(8,128)(2,1)} %param.9) | copy-start | bytes 9437188
  207.1 6.3 %copy-start.4 = (bf16[1,2,384,2048]{3,2,1,0:T(8,128)(2,1)S(1)}, bf16[1,2,384,2048]{3,2,1,0:T(8,128)(2,1)}, u32[]{:S(2)}) copy-start(bf16[1,2,384,2048]{3,2,1,0:T(8,128)(2,1)} %param.10) | copy-start | bytes 9437188
  213.4 101.5 %copy-start.1 = (bf16[1,2,384,1536]{3,2,1,0:T(8,128)(2,1)S(1)}, bf16[1,2,384,1536]{3,2,1,0:T(8,128)(2,1)}, u32[]{:S(2)}) copy-start(bf16[1,2,384,1536]{3,2,1,0:T(8,128)(2,1)} %param.12) | copy-start | bytes 7077892
  214.2 44.0 %collective-permute-start = (bf16[384,2048]{1,0:T(8,128)(2,1)S(1)}, bf16[384,2048]{1,0:T(8,128)(2,1)}, u32[]{:S(2)}, u32[]{:S(2)}) collective-permute-start(bf16[384,2048]{1,0:T(8,128)(2,1)S(1)} %fusion.22), channel_id=1, source_target_pairs={{0,240},{16,0},{32,16},{48,32},{64,48},{80,64},{96,80},{112,96},{1... | collective-permute-start | bytes 4718600 | tf_op jit(solution)/shard_map/ppermute | solution.py:17
Sparse Core Ops, SparseCore 0:
  11.6 141.8 all-gather.2
Sparse Core Ops, SparseCore 1:
  15.9 21.8 reduce-scatter.5
  42.1 129.5 reduce-scatter.3
  192.8 117.6 reduce-scatter.7
